TPU v7x, 32 devices: a whole 2x2x4 slice. The times are simulated.
32 devices in a mesh: tile: 8 (over z, y), band: 4 (over x, core).
Axes of the slice: x: 2, y: 2, z: 4, core: 2. Of those that a mesh axis runs over, the one named last changes fastest.
Arguments:
- observed: float32 [96, 4096, 128], P('band', 'tile'), may hold values from 0 to 4
- weights: float32 [96, 4096, 128], P('band', 'tile'), may hold values from 0.2 to 6, as said below
- morphology: float32 [4, 4096, 128], P(None, 'tile'), may hold values from 0 to 1
- spectra: float32 [4, 96, 2048], P(None, 'band', 'tile'), may hold values from 0.2 to 2
- blend_blocks: int32 [8, 256], P('tile'), may hold values from 1 to 4, 512 in all within a row
- source_count: int32 [2048], P('tile'), may hold values from 1 to 4
- sent_blocks: int32 [8, 8, 4], P('tile'), may hold values from 0 to 512, as said below
- landing_blocks: int32 [8, 8, 4], P('tile'), may hold values from 0 to 512, as said below
Outputs:
- new_morphology: float32 [4, 4096, 128], P(None, 'tile')
- new_spectra: float32 [4, 96, 2048], P(None, 'band', 'tile')
- misfit: float32 [2048], P('tile')
Inputs may be any that keep to these rules, and one draw needn't show every extreme that they name: `weights`: Positive. `sent_blocks`: entry [s, d, j] is a block of tile index s whose model margins a block of tile index d, or 512 for an empty slot; at most 4 live slots from one sender to one receiver, the live ones first; every sender fills all 4 slots to some receiver and every receiver gets all 4 from some sender; a block may appear in several slots. `landing_blocks`: entry [d, s, j] is the block of tile index d on which slot j from sender s lands, or 512 exactly where sent_blocks[s, d, j] is 512; several slots may land on one block.
All inputs are finite; a program needn't handle non-finite values.
Results may differ from a plain program's by a relative error of at most 0.0003.
Values sent between devices are 32-bit elements; how exact they have to be, the bound alone decides.
A program may use at most 128 MiB of HBM per device.

v0:
```python
import functools
import jax
import jax.numpy as jnp
from jax import lax
from jax.experimental import pallas as pl
from jax.experimental.pallas import tpu as pltpu
from jax.sharding import PartitionSpec as P

ITERS = 2
LANES = 128
SUB = 8
MESH = pl.DeviceIdType.MESH
VM = pl.BlockSpec(memory_space=pltpu.VMEM)
F32 = jnp.float32
BF = jnp.bfloat16


def split2(x):
    hi = x.astype(BF)
    return hi, (x - hi.astype(F32)).astype(BF)


def split3(x):
    hi = x.astype(BF)
    rest = x - hi.astype(F32)
    mid = rest.astype(BF)
    return hi, mid, (rest - mid.astype(F32)).astype(BF)


NN = ((1,), (0,))
NT = ((1,), (1,))
TN = ((0,), (0,))


def select_dot(x, onehot, dims):
    out = None
    for piece in split3(x):
        part = lax.dot_general(piece, onehot, (dims, ((), ())), preferred_element_type=F32)
        out = part if out is None else out + part
    return out


def pick_dot(onehot, x):
    out = None
    for piece in split3(x):
        part = lax.dot_general(onehot, piece, (NT, ((), ())), preferred_element_type=F32)
        out = part if out is None else out + part
    return out


def write_packets(sent_ref, shape_ref, cb_ref, pkt_ref):
    sources = shape_ref.shape[0]
    slots = pkt_ref.shape[0]
    pkt_ref[...] = jnp.zeros_like(pkt_ref)
    sent = sent_ref[...]
    for k in range(sources):
        pkt_ref[:, k, :] = pick_dot(sent, shape_ref[k])[:slots]
    pkt_ref[:, sources, :] = pick_dot(sent, cb_ref[...])[:slots]


def start_kernel(chan, sent_ref, morph_ref, spec_ref, len_ref, cnt_ref,
                 shape_ref, color_ref, cb_ref, memt_ref, cntb_ref, amask_ref, pkt_ref):
    sources, blocks, _ = morph_ref.shape
    blends = len_ref.shape[1]
    lengths = jnp.broadcast_to(len_ref[...].astype(F32), (SUB, blends))
    rows = lax.broadcasted_iota(jnp.int32, (blends, blends), 0)
    cols = lax.broadcasted_iota(jnp.int32, (blends, blends), 1)
    ends = jnp.dot(lengths.astype(BF), (rows <= cols).astype(F32).astype(BF), preferred_element_type=F32)
    starts = ends - lengths
    pos = lax.broadcasted_iota(jnp.int32, (blocks, blends), 0).astype(F32)
    memt = jnp.where((pos >= starts[0:1]) & (pos < ends[0:1]), 1.0, 0.0).astype(BF)
    memt_ref[...] = memt
    count = jnp.broadcast_to(cnt_ref[...].astype(F32), (SUB, blends))
    count_b = lax.dot_general(count.astype(BF), memt, (NT, ((), ())), preferred_element_type=F32)
    cntb_ref[...] = count_b
    row = lax.broadcasted_iota(jnp.int32, (LANES, blends), 0)
    amask = jnp.where(((row // chan).astype(F32) < count[0:1]) & (row < chan * sources), 1.0, 0.0)
    amask_ref[...] = amask
    color = spec_ref[...] * amask
    color_ref[...] = color
    cb_ref[...] = select_dot(color, memt, NT)
    for k in range(sources):
        shape_ref[k] = jnp.transpose(morph_ref[k]) * jnp.where(count_b[0:1] > k, 1.0, 0.0)
    write_packets(sent_ref, shape_ref, cb_ref, pkt_ref)


def exchange_kernel(tiles, src_ref, out_ref, land, send_sem, recv_sem):
    me = lax.axis_index("tile")
    slots = src_ref.shape[0] // tiles
    barrier = pltpu.get_barrier_semaphore()
    for o in range(1, tiles):
        pl.semaphore_signal(barrier, inc=1, device_id={"tile": lax.rem(me + o, tiles)}, device_id_type=MESH)
    pl.semaphore_wait(barrier, tiles - 1)
    copies = []
    for o in range(1, tiles):
        to = lax.rem(me + o, tiles)
        copy = pltpu.make_async_remote_copy(
            src_ref=src_ref.at[pl.ds(to * slots, slots)],
            dst_ref=land.at[pl.ds(me * slots, slots)],
            send_sem=send_sem.at[o], recv_sem=recv_sem.at[o],
            device_id={"tile": to}, device_id_type=MESH)
        copy.start()
        copies.append(copy)
    land[pl.ds(me * slots, slots)] = src_ref[pl.ds(me * slots, slots)]
    for o in range(1, tiles):
        frm = lax.rem(me - o + tiles, tiles)
        pltpu.make_async_remote_copy(
            src_ref=src_ref.at[pl.ds(frm * slots, slots)],
            dst_ref=land.at[pl.ds(frm * slots, slots)],
            send_sem=send_sem.at[o], recv_sem=recv_sem.at[o],
            device_id={"tile": frm}, device_id_type=MESH).wait_recv()
    out_ref[...] = land[...]
    for copy in copies:
        copy.wait_send()


def exchange(packets, tiles, cid):
    return pl.pallas_call(
        functools.partial(exchange_kernel, tiles),
        out_shape=jax.ShapeDtypeStruct(packets.shape, F32),
        in_specs=[VM], out_specs=VM,
        scratch_shapes=[pltpu.VMEM(packets.shape, F32), pltpu.SemaphoreType.DMA((tiles,)),
                        pltpu.SemaphoreType.DMA((tiles,))],
        compiler_params=pltpu.CompilerParams(collective_id=cid, has_side_effects=True),
    )(packets)


def fold(x):
    return jnp.sum(x.reshape(x.shape[0] // SUB, SUB, x.shape[1]), axis=0)


def column(ref, index, rows):
    return jnp.broadcast_to(ref[pl.ds(index, 1), :], (rows, LANES))


def main_kernel(sources, hit_ref, recv_ref, obs_ref, wts_ref, shape_ref, cb_ref,
                grad_ref, pb_ref, aux_ref, ret_ref, incm, adjs, wtt, wl, pbs, vsh, vcol, mis, vpb):
    chan, rows, pixels = obs_ref.shape
    slots = recv_ref.shape[0]
    step = pl.program_id(0)
    kc = sources * chan
    deep = 32

    @pl.when(step == 0)
    def _():
        wl[...] = jnp.zeros_like(wl)

        def padded(x):
            if slots < LANES:
                x = jnp.concatenate([x, jnp.zeros((LANES - slots, LANES), F32)], axis=0)
            return jnp.transpose(x)

        for k in range(sources):
            vsh[k] = padded(recv_ref[:, k, :])
        vcol[...] = padded(recv_ref[:, sources, :])
        for c in range(chan):
            own = None
            for k in range(sources):
                term = column(vcol, k * chan + c, pixels) * vsh[k]
                own = term if own is None else own + term
            hi, lo = split2(own)
            incm[c] = jnp.concatenate([hi, lo], axis=1)

    hit = hit_ref[...]
    hit2 = jnp.concatenate([hit, hit], axis=0)
    for c in range(chan):
        inc = jnp.dot(incm[c], hit2, preferred_element_type=F32)
        adjs[c] = inc - jnp.transpose(obs_ref[c])
        wtt[c] = jnp.transpose(wts_ref[c])
    pbs[...] = jnp.zeros_like(pbs)
    mis[...] = jnp.zeros_like(mis)

    def slab(g, carry):
        at = pl.ds(pl.multiple_of(g * deep, deep), deep)
        sh = [shape_ref[k, at, :] for k in range(sources)]
        grads = [None] * sources
        for c in range(chan):
            cols = [column(cb_ref, k * chan + c, deep) for k in range(sources)]
            own = adjs[c, at, :]
            for k in range(sources):
                own = own + cols[k] * sh[k]
            adj = wtt[c, at, :] * own
            adjs[c, at, :] = adj
            mis[0] += fold(adj * own)
            for k in range(sources):
                term = cols[k] * adj
                grads[k] = term if grads[k] is None else grads[k] + term
                pbs[k * chan + c] += fold(sh[k] * adj)
        for k in range(sources):
            grad_ref[k, at, :] = grads[k]
            mis[1 + k] += fold(sh[k] * sh[k])
        return carry

    lax.fori_loop(0, pixels // deep, slab, 0)
    pb_ref[...] = jnp.zeros_like(pb_ref)
    pb_ref[pl.ds(0, kc), :] = jnp.sum(pbs[...], axis=1)
    aux_ref[...] = jnp.zeros_like(aux_ref)
    total = jnp.sum(mis[...], axis=1)
    aux_ref[pl.ds(sources, 1), :] = total[0:1]
    aux_ref[pl.ds(SUB, sources), :] = total[1:1 + sources]
    for k in range(sources):
        mine = cb_ref[pl.ds(k * chan, chan), :]
        aux_ref[pl.ds(k, 1), :] = jnp.sum(mine * mine, axis=0, keepdims=True)
    hit_wide = jnp.concatenate([hit, hit], axis=1)
    for c in range(chan):
        hi, lo = split2(adjs[c])
        wl[c] += lax.dot_general(jnp.concatenate([hi, lo], axis=1), hit_wide, (NT, ((), ())),
                                 preferred_element_type=F32)

    @pl.when(step == pl.num_programs(0) - 1)
    def _():
        ret_ref[...] = jnp.zeros_like(ret_ref)
        vpb[...] = jnp.zeros_like(vpb)
        pbs[...] = jnp.zeros_like(pbs)

        def back(g, carry):
            at = pl.ds(pl.multiple_of(g * deep, deep), deep)
            sh = [vsh[k, at, :] for k in range(sources)]
            grads = [None] * sources
            for c in range(chan):
                adj = wl[c, at, :]
                for k in range(sources):
                    term = column(vcol, k * chan + c, deep) * adj
                    grads[k] = term if grads[k] is None else grads[k] + term
                    pbs[k * chan + c] += fold(sh[k] * adj)
            for k in range(sources):
                vsh[k, at, :] = grads[k]
            return carry

        lax.fori_loop(0, pixels // deep, back, 0)
        vpb[pl.ds(0, kc), :] = jnp.sum(pbs[...], axis=1)
        for k in range(sources):
            ret_ref[:, k, :] = jnp.transpose(vsh[k])[:slots]
        ret_ref[:, sources, :] = jnp.transpose(vpb[...])[:slots]


def main_pass(hit, recv, observed, weights, shape_now, cb):
    sources, pixels, blocks = shape_now.shape
    chan = observed.shape[0]
    slots = recv.shape[0]
    rows = LANES
    big = pl.BlockSpec((chan, rows, pixels), lambda i: (0, i, 0))
    whole = pl.BlockSpec(recv.shape, lambda i: (0, 0, 0))
    table = pl.BlockSpec((LANES, rows), lambda i: (0, i))
    shp = pl.BlockSpec((sources, pixels, rows), lambda i: (0, 0, i))
    sds = jax.ShapeDtypeStruct
    slab = pltpu.VMEM((chan, pixels, LANES), F32)
    return pl.pallas_call(
        functools.partial(main_kernel, sources),
        grid=(blocks // rows,),
        in_specs=[table, whole, big, big, shp, table],
        out_specs=[shp, table, pl.BlockSpec((2 * SUB, rows), lambda i: (0, i)), whole],
        out_shape=[sds(shape_now.shape, F32), sds((LANES, blocks), F32), sds((2 * SUB, blocks), F32),
                   sds(recv.shape, F32)],
        scratch_shapes=[pltpu.VMEM((chan, pixels, 2 * LANES), BF), slab, slab, slab,
                        pltpu.VMEM((sources * chan, SUB, LANES), F32),
                        pltpu.VMEM((sources, pixels, LANES), F32), pltpu.VMEM((LANES, LANES), F32),
                        pltpu.VMEM((SUB, SUB, LANES), F32), pltpu.VMEM((LANES, LANES), F32)],
        compiler_params=pltpu.CompilerParams(dimension_semantics=("arbitrary",)),
    )(hit, recv, observed, weights, shape_now, cb)


def fix_kernel(chan, sent_ref, back_ref, grad_ref, pb_ref, aux_ref, memt_ref, color_ref, amask_ref,
               gout_ref, auxt_ref, cnext_ref):
    sources = grad_ref.shape[0]
    slots = back_ref.shape[0]
    sent = sent_ref[...][:slots]
    for k in range(sources):
        gout_ref[k] = grad_ref[k] + select_dot(back_ref[:, k, :], sent, TN)
    per_block = pb_ref[...] + select_dot(back_ref[:, sources, :], sent, TN)
    auxt_ref[...] = aux_ref[pl.ds(0, SUB), :]
    memt = memt_ref[...]
    grad_color = select_dot(per_block, memt, NN)
    powers = select_dot(aux_ref[pl.ds(SUB, SUB), :], memt, NN)
    row = lax.broadcasted_iota(jnp.int32, color_ref.shape, 0) // chan
    power = jnp.zeros(color_ref.shape, F32)
    for k in range(sources):
        power = jnp.where(row == k, powers[k:k + 1], power)
    cnext_ref[...] = jnp.maximum(color_ref[...] - grad_color / (1.0 + power), 0.0) * amask_ref[...]


def reduce_kernel(bands, parts, g_ref, a_ref, gout_ref, aout_ref, r1, r2, r3, ar,
                  s1, v1, s2, v2, s3, v3, sa, va):
    me = lax.axis_index("band")
    core = lax.rem(me, 2)
    x = me // 2
    chips = bands // 2
    partner = x * 2 + 1 - core
    half = g_ref.shape[1] // 2
    rows = half // parts
    barrier = pltpu.get_barrier_semaphore()
    for o in range(1, bands):
        pl.semaphore_signal(barrier, inc=1, device_id={"band": lax.rem(me + o, bands)}, device_id_type=MESH)
    pl.semaphore_wait(barrier, bands - 1)

    def chunk(c, q):
        return pl.ds(pl.multiple_of(c * half + q * rows, SUB), rows)

    sends = []
    for q in range(parts):
        copy = pltpu.make_async_remote_copy(
            src_ref=g_ref.at[:, chunk(1 - core, q), :], dst_ref=r1.at[q],
            send_sem=s1.at[q], recv_sem=v1.at[q], device_id={"band": partner}, device_id_type=MESH)
        copy.start()
        sends.append(copy)
    first = list(sends)
    for o in range(1, bands):
        to = lax.rem(me + o, bands)
        copy = pltpu.make_async_remote_copy(
            src_ref=a_ref, dst_ref=ar.at[me], send_sem=sa.at[o], recv_sem=va.at[o],
            device_id={"band": to}, device_id_type=MESH)
        copy.start()
        sends.append(copy)
    ar[me] = a_ref[...]
    for q in range(parts):
        first[q].wait_recv()
        r2[x, q] = g_ref[:, chunk(core, q), :] + r1[q]
        for o in range(1, chips):
            to = lax.rem(x + o, chips)
            copy = pltpu.make_async_remote_copy(
                src_ref=r2.at[x, q], dst_ref=r2.at[x, q], send_sem=s2.at[o, q], recv_sem=v2.at[o, q],
                device_id={"band": to * 2 + core}, device_id_type=MESH)
            copy.start()
            sends.append(copy)
    last = []
    for q in range(parts):
        for o in range(1, chips):
            frm = lax.rem(x - o + chips, chips)
            pltpu.make_async_remote_copy(
                src_ref=r2.at[frm, q], dst_ref=r2.at[frm, q], send_sem=s2.at[o, q], recv_sem=v2.at[o, q],
                device_id={"band": frm * 2 + core}, device_id_type=MESH).wait_recv()
        total = r2[0, q]
        for i in range(1, chips):
            total = total + r2[i, q]
        gout_ref[:, chunk(core, q), :] = total
        copy = pltpu.make_async_remote_copy(
            src_ref=gout_ref.at[:, chunk(core, q), :], dst_ref=r3.at[q],
            send_sem=s3.at[q], recv_sem=v3.at[q], device_id={"band": partner}, device_id_type=MESH)
        copy.start()
        last.append(copy)
    for o in range(1, bands):
        frm = lax.rem(me - o + bands, bands)
        pltpu.make_async_remote_copy(
            src_ref=a_ref, dst_ref=ar.at[frm], send_sem=sa.at[o], recv_sem=va.at[o],
            device_id={"band": frm}, device_id_type=MESH).wait_recv()
    total = ar[0]
    for i in range(1, bands):
        total = total + ar[i]
    aout_ref[...] = total
    for q in range(parts):
        last[q].wait_recv()
        gout_ref[:, chunk(1 - core, q), :] = r3[q]
    for copy in sends + last:
        copy.wait_send()


def band_sum(grad, auxt, bands, cid):
    sources, pixels, lanes = grad.shape
    parts = 4
    rows = pixels // 2 // parts
    chips = bands // 2
    dma = pltpu.SemaphoreType.DMA
    return pl.pallas_call(
        functools.partial(reduce_kernel, bands, parts),
        out_shape=[jax.ShapeDtypeStruct(grad.shape, F32), jax.ShapeDtypeStruct(auxt.shape, F32)],
        in_specs=[VM, VM], out_specs=[VM, VM],
        scratch_shapes=[pltpu.VMEM((parts, sources, rows, lanes), F32),
                        pltpu.VMEM((chips, parts, sources, rows, lanes), F32),
                        pltpu.VMEM((parts, sources, rows, lanes), F32),
                        pltpu.VMEM((bands,) + auxt.shape, F32),
                        dma((parts,)), dma((parts,)), dma((chips, parts)), dma((chips, parts)),
                        dma((parts,)), dma((parts,)), dma((bands,)), dma((bands,))],
        compiler_params=pltpu.CompilerParams(collective_id=cid, has_side_effects=True),
    )(grad, auxt)


def step_kernel(final, sent_ref, shape_ref, grad_ref, auxt_ref, cntb_ref, memt_ref, color_ref, *outs):
    sources = shape_ref.shape[0]
    snext_ref = outs[0]
    for k in range(sources):
        step = 1.0 / (1.0 + auxt_ref[pl.ds(k, 1), :])
        alive = jnp.where(cntb_ref[pl.ds(0, 1), :] > k, 1.0, 0.0)
        shape = jnp.maximum(shape_ref[k] - step * grad_ref[k], 0.0) * alive
        snext_ref[k] = jnp.transpose(shape) if final else shape
    if final:
        outs[1][...] = select_dot(auxt_ref[...], memt_ref[...], NN)
    else:
        outs[1][...] = select_dot(color_ref[...], memt_ref[...], NT)
        write_packets(sent_ref, snext_ref, outs[1], outs[2])


def on_device(
    observed, weights, morphology, spectra, blend_blocks, source_count, sent_blocks, landing_blocks
):
    chan, blocks, pixels = observed.shape
    sources = morphology.shape[0]
    blends = spectra.shape[2]
    tiles = lax.axis_size("tile")
    bands = lax.axis_size("band")
    slots = tiles * sent_blocks.shape[2]

    def onehot(index):
        index = jnp.pad(index.reshape(-1), (0, LANES - slots), constant_values=blocks)
        return (index[:, None] == jnp.arange(blocks, dtype=jnp.int32)[None, :]).astype(BF)

    sent = onehot(sent_blocks)
    hit = onehot(landing_blocks)
    spec2 = jnp.pad(spectra.reshape(sources * chan, blends), ((0, LANES - sources * chan), (0, 0)))
    sds = jax.ShapeDtypeStruct
    packet = sds((slots, SUB, LANES), F32)
    table = sds((LANES, blocks), F32)
    palette = sds((LANES, blends), F32)
    turned = sds((sources, pixels, blocks), F32)
    shape_now, color_now, cb, memt, cntb, amask, packets = pl.pallas_call(
        functools.partial(start_kernel, chan),
        in_specs=[VM] * 5, out_specs=[VM] * 7,
        out_shape=[turned, palette, table, sds((blocks, blends), BF), sds((SUB, blocks), F32), palette, packet],
    )(sent, morphology, spec2, blend_blocks, source_count.reshape(1, blends))
    for it in range(ITERS):
        recv = exchange(packets, tiles, 3 * it)
        grad, pb, aux, ret = main_pass(hit, recv, observed, weights, shape_now, cb)
        back = exchange(ret, tiles, 3 * it + 1)
        grad, auxt, color_now = pl.pallas_call(
            functools.partial(fix_kernel, chan),
            in_specs=[VM] * 8, out_specs=[VM] * 3,
            out_shape=[turned, sds((SUB, blocks), F32), palette],
        )(sent, back, grad, pb, aux, memt, color_now, amask)
        grad, auxt = band_sum(grad, auxt, bands, 3 * it + 2)
        final = it == ITERS - 1
        outs = [sds(morphology.shape, F32), sds((SUB, blends), F32)] if final else [turned, table, packet]
        results = pl.pallas_call(
            functools.partial(step_kernel, final),
            in_specs=[VM] * 7, out_specs=[VM] * len(outs), out_shape=outs,
        )(sent, shape_now, grad, auxt, cntb, memt, color_now)
        if not final:
            shape_now, cb, packets = results
    spectra_out = color_now[:sources * chan].reshape(sources, chan, blends)
    return (results[0], spectra_out, results[1][sources])


def solution(mesh):
    return jax.shard_map(
        on_device,
        mesh=mesh,
        in_specs=(
            P("band", "tile", None),
            P("band", "tile", None),
            P(None, "tile", None),
            P(None, "band", "tile"),
            P("tile", None),
            P("tile"),
            P("tile", None, None),
            P("tile", None, None),
        ),
        out_specs=(P(None, "tile", None), P(None, "band", "tile"), P("tile")),
        check_vma=False,
    )
```

profile of v0, /device:TPU:0, one launch (start us, length us, event | category | flops | bytes accessed | tf_op | source)
XLA Modules:
  0.0 133.9 jit_solution(8380207863010276891)
XLA Ops:
  0.6 0.8 copy.13
  1.4 0.1 reshape.23
  1.5 0.8 copy.14
  2.2 0.1 reshape.26
  2.3 0.7 fusion.sent_ref
  3.1 0.7 fusion.1.hit_ref
  3.8 1.5 %pad.12.spec_ref = f32[128,256]{1,0:T(8,128)} pad(f32[96,256]{1,0:T(8,128)} %bitcast.4, f32[]{:T(128)} %constant.4.clone.1), padding=0_32x0_0 | pad | bytes 229380 | tf_op jit(solution)/shard_map/jit(_pad)/pad | solution.py:408
  5.4 3.1 %shard_map.103 = (f32[4,128,512]{2,1,0:T(8,128)}, f32[128,256]{1,0:T(8,128)}, f32[128,512]{1,0:T(8,128)}, bf16[512,256]{1,0:T(8,128)(2,1)}, f32[8,512]{1,0:T(8,1...) custom-call(bf16[128,512]{1,0:T(8,128)(2,1)} %fusion.sent_ref, f32[4,512,128]{2,1,0:T(8,128)} %morph_ref.1, ...), custom_call_target="tpu_custom_call" | custom-call | tf_op jit(solution)/shard_map/pallas_call | solution.py:414
  8.4 10.9 %shard_map.104.recv_ref = f32[32,8,128]{2,1,0:T(8,128)} custom-call(f32[32,8,128]{2,1,0:T(8,128)} %get-tuple-element.34.src_ref), custom_call_target="tpu_custom_call" | custom-call | tf_op jit(solution)/shard_map/pallas_call | solution.py:118
  19.3 16.6 %shard_map.105 = (f32[4,128,512]{2,1,0:T(8,128)}, f32[128,512]{1,0:T(8,128)}, f32[16,512]{1,0:T(8,128)}, f32[32,8,128]{2,1,0:T(8,128)}) custom-call(bf16[128,512]{1,0:T(8,128)(2,1)} %fusion.1.hit_ref, f32[32,8,128]{2,1,0:T(8,128)} %shard_map.104.recv_ref, f32[24,512,128]{2,1,0:T(8,128)} %obs_ref.3, f32[24,512,128]{2,1,0:T(8,128)} %wts_ref.3, ...), custom_call_target="tpu_custom_call" | custom-call | tf_op jit(solution)/shard_map/pallas_call | solution.py:248
  36.0 8.9 %shard_map.106.back_ref = f32[32,8,128]{2,1,0:T(8,128)} custom-call(f32[32,8,128]{2,1,0:T(8,128)} %get-tuple-element.36.src_ref), custom_call_target="tpu_custom_call" | custom-call | tf_op jit(solution)/shard_map/pallas_call | solution.py:118
  44.9 3.3 %shard_map.107 = (f32[4,128,512]{2,1,0:T(8,128)}, f32[8,512]{1,0:T(8,128)}, f32[128,256]{1,0:T(8,128)}) custom-call(bf16[128,512]{1,0:T(8,128)(2,1)} %fusion.sent_ref, f32[32,8,128]{2,1,0:T(8,128)} %shard_map.106.back_ref, f32[4,128,512]{2,1,0:T(8,128)} %get-tuple-element.37.grad_ref, f32[128,512]{1,0:T(8,128)} %get-tuple-element.38.pb_ref, ...), custom_call_target="tpu_custom_call" | custom-call | tf_op jit(solution)/shard_map/pallas_call | solution.py:423
  48.1 19.1 %shard_map.108 = (f32[4,128,512]{2,1,0:T(8,128)}, f32[8,512]{1,0:T(8,128)}) custom-call(f32[4,128,512]{2,1,0:T(8,128)} %get-tuple-element.43.g_ref, f32[8,512]{1,0:T(8,128)} %get-tuple-element.44.a_ref), custom_call_target="tpu_custom_call" | custom-call | tf_op jit(solution)/shard_map/pallas_call | solution.py:363
  67.2 3.3 %shard_map.109 = (f32[4,128,512]{2,1,0:T(8,128)}, f32[128,512]{1,0:T(8,128)}, f32[32,8,128]{2,1,0:T(8,128)}) custom-call(bf16[128,512]{1,0:T(8,128)(2,1)} %fusion.sent_ref, f32[4,128,512]{2,1,0:T(8,128)} %get-tuple-element.33.shape_ref, f32[4,128,512]{2,1,0:T(8,128)} %get-tuple-element.45.grad_ref, f32[8,512]{1,0:T(8,128)} %get-tuple-element.46.auxt_ref, ...), custom_call_target="tpu_custom_call" | custom-call | tf_op jit(solution)/shard_map/pallas_call | solution.py:431
  70.5 9.6 %shard_map.110.recv_ref = f32[32,8,128]{2,1,0:T(8,128)} custom-call(f32[32,8,128]{2,1,0:T(8,128)} %get-tuple-element.50.src_ref), custom_call_target="tpu_custom_call" | custom-call | tf_op jit(solution)/shard_map/pallas_call | solution.py:118
  80.1 16.7 %shard_map.111 = (f32[4,128,512]{2,1,0:T(8,128)}, f32[128,512]{1,0:T(8,128)}, f32[16,512]{1,0:T(8,128)}, f32[32,8,128]{2,1,0:T(8,128)}) custom-call(bf16[128,512]{1,0:T(8,128)(2,1)} %fusion.1.hit_ref, f32[32,8,128]{2,1,0:T(8,128)} %shard_map.110.recv_ref, f32[24,512,128]{2,1,0:T(8,128)} %obs_ref.3, f32[24,512,128]{2,1,0:T(8,128)} %wts_ref.3, ...), custom_call_target="tpu_custom_call" | custom-call | tf_op jit(solution)/shard_map/pallas_call | solution.py:248
  96.8 9.0 %shard_map.112.back_ref = f32[32,8,128]{2,1,0:T(8,128)} custom-call(f32[32,8,128]{2,1,0:T(8,128)} %get-tuple-element.52.src_ref), custom_call_target="tpu_custom_call" | custom-call | tf_op jit(solution)/shard_map/pallas_call | solution.py:118
  105.7 3.2 %shard_map.113 = (f32[4,128,512]{2,1,0:T(8,128)}, f32[8,512]{1,0:T(8,128)}, f32[128,256]{1,0:T(8,128)}) custom-call(bf16[128,512]{1,0:T(8,128)(2,1)} %fusion.sent_ref, f32[32,8,128]{2,1,0:T(8,128)} %shard_map.112.back_ref, f32[4,128,512]{2,1,0:T(8,128)} %get-tuple-element.53.grad_ref, f32[128,512]{1,0:T(8,128)} %get-tuple-element.54.pb_ref, ...), custom_call_target="tpu_custom_call" | custom-call | tf_op jit(solution)/shard_map/pallas_call | solution.py:423
  109.0 19.0 %shard_map.114 = (f32[4,128,512]{2,1,0:T(8,128)}, f32[8,512]{1,0:T(8,128)}) custom-call(f32[4,128,512]{2,1,0:T(8,128)} %get-tuple-element.56.g_ref, f32[8,512]{1,0:T(8,128)} %get-tuple-element.57.a_ref), custom_call_target="tpu_custom_call" | custom-call | tf_op jit(solution)/shard_map/pallas_call | solution.py:363
  128.0 3.0 %shard_map.115 = (f32[4,512,128]{2,1,0:T(8,128)}, f32[8,256]{1,0:T(8,128)}) custom-call(bf16[128,512]{1,0:T(8,128)(2,1)} %fusion.sent_ref, f32[4,128,512]{2,1,0:T(8,128)} %get-tuple-element.49.shape_ref, f32[4,128,512]{2,1,0:T(8,128)} %get-tuple-element.58.grad_ref, f32[8,512]{1,0:T(8,128)} %get-tuple-element.59.auxt_ref, ...), custom_call_target="tpu_custom_call" | custom-call | tf_op jit(solution)/shard_map/pallas_call | solution.py:431
  131.1 1.5 %slice.6 = f32[96,256]{1,0:T(8,128)} slice(f32[128,256]{1,0:T(8,128)} %get-tuple-element.60.color_ref), slice={[0:96], [0:256]} | slice | bytes 196608 | tf_op jit(solution)/shard_map/slice | solution.py:437
  132.6 1.3 slice.7
  (2 shorter events, 0.0 us)
where the time goes:
time: 134 us
  Pallas kernels  126 us (94%)
  local copies, waits for them, and re-layouts  6.04 us (5%)
  other arithmetic  1.48 us (1%)
    pallas_call x4, Pallas kernels, exchange(): pl.pallas_call(functools.partial(exchange_kernel, tiles), out_shape=jax.S...  38.3 us
    pallas_call x2, Pallas kernels, band_sum(): pl.pallas_call(functools.partial(reduce_kernel, bands, parts), out_shape=...  38.1 us
    pallas_call x2, Pallas kernels, main_pass(): pl.pallas_call(functools.partial(main_kernel, sources), grid=(blocks // r...  33.3 us
    pallas_call x2, Pallas kernels, on_device(): pl.pallas_call(functools.partial(fix_kernel, chan), in_specs=[VM] * 8, ou...  6.5 us
    pallas_call x2, Pallas kernels, on_device(): pl.pallas_call(functools.partial(step_kernel, final), in_specs=[VM] * 7,...  6.32 us
    pallas_call x1, Pallas kernels, on_device(): pl.pallas_call(functools.partial(start_kernel, chan), in_specs=[VM] * 5,...  3.08 us

commit v1 on v0

--- a/solution.py
+++ b/solution.py
@@ -260,27 +260,10 @@
     )(hit, recv, observed, weights, shape_now, cb)
 
 
-def fix_kernel(chan, sent_ref, back_ref, grad_ref, pb_ref, aux_ref, memt_ref, color_ref, amask_ref,
-               gout_ref, auxt_ref, cnext_ref):
-    sources = grad_ref.shape[0]
-    slots = back_ref.shape[0]
-    sent = sent_ref[...][:slots]
-    for k in range(sources):
-        gout_ref[k] = grad_ref[k] + select_dot(back_ref[:, k, :], sent, TN)
-    per_block = pb_ref[...] + select_dot(back_ref[:, sources, :], sent, TN)
-    auxt_ref[...] = aux_ref[pl.ds(0, SUB), :]
-    memt = memt_ref[...]
-    grad_color = select_dot(per_block, memt, NN)
-    powers = select_dot(aux_ref[pl.ds(SUB, SUB), :], memt, NN)
-    row = lax.broadcasted_iota(jnp.int32, color_ref.shape, 0) // chan
-    power = jnp.zeros(color_ref.shape, F32)
-    for k in range(sources):
-        power = jnp.where(row == k, powers[k:k + 1], power)
-    cnext_ref[...] = jnp.maximum(color_ref[...] - grad_color / (1.0 + power), 0.0) * amask_ref[...]
-
-
-def reduce_kernel(bands, parts, g_ref, a_ref, gout_ref, aout_ref, r1, r2, r3, ar,
-                  s1, v1, s2, v2, s3, v3, sa, va):
+def reduce_kernel(tiles, bands, parts, src_ref, g_ref, a_ref, gout_ref, aout_ref, sum_ref, own_ref,
+                  r1, r2, r3, ar, land, b1, b2, s1, v1, s2, v2, s3, v3, sa, va, st, vt, sb, vb, sc, vc):
+    spot = lax.axis_index("tile")
+    slots = src_ref.shape[0] // tiles
     me = lax.axis_index("band")
     core = lax.rem(me, 2)
     x = me // 2
@@ -291,7 +274,9 @@
     barrier = pltpu.get_barrier_semaphore()
     for o in range(1, bands):
         pl.semaphore_signal(barrier, inc=1, device_id={"band": lax.rem(me + o, bands)}, device_id_type=MESH)
-    pl.semaphore_wait(barrier, bands - 1)
+    for o in range(1, tiles):
+        pl.semaphore_signal(barrier, inc=1, device_id={"tile": lax.rem(spot + o, tiles)}, device_id_type=MESH)
+    pl.semaphore_wait(barrier, bands + tiles - 2)
 
     def chunk(c, q):
         return pl.ds(pl.multiple_of(c * half + q * rows, SUB), rows)
@@ -304,14 +289,22 @@
         copy.start()
         sends.append(copy)
     first = list(sends)
+    for o in range(1, tiles):
+        to = lax.rem(spot + o, tiles)
+        copy = pltpu.make_async_remote_copy(
+            src_ref=src_ref.at[pl.ds(to * slots, slots)], dst_ref=land.at[pl.ds(spot * slots, slots)],
+            send_sem=st.at[o], recv_sem=vt.at[o], device_id={"tile": to}, device_id_type=MESH)
+        copy.start()
+        sends.append(copy)
+    land[pl.ds(spot * slots, slots)] = src_ref[pl.ds(spot * slots, slots)]
     for o in range(1, bands):
         to = lax.rem(me + o, bands)
         copy = pltpu.make_async_remote_copy(
-            src_ref=a_ref, dst_ref=ar.at[me], send_sem=sa.at[o], recv_sem=va.at[o],
+            src_ref=a_ref.at[pl.ds(0, SUB)], dst_ref=ar.at[me], send_sem=sa.at[o], recv_sem=va.at[o],
             device_id={"band": to}, device_id_type=MESH)
         copy.start()
         sends.append(copy)
-    ar[me] = a_ref[...]
+    ar[me] = a_ref[pl.ds(0, SUB), :]
     for q in range(parts):
         first[q].wait_recv()
         r2[x, q] = g_ref[:, chunk(core, q), :] + r1[q]
@@ -323,7 +316,31 @@
             copy.start()
             sends.append(copy)
     last = []
+    pair = None
     for q in range(parts):
+        if q == parts // 2:
+            for o in range(1, tiles):
+                frm = lax.rem(spot - o + tiles, tiles)
+                pltpu.make_async_remote_copy(
+                    src_ref=src_ref.at[pl.ds(frm * slots, slots)], dst_ref=land.at[pl.ds(frm * slots, slots)],
+                    send_sem=st.at[o], recv_sem=vt.at[o], device_id={"tile": frm},
+                    device_id_type=MESH).wait_recv()
+            pair = pltpu.make_async_remote_copy(
+                src_ref=land, dst_ref=b1, send_sem=sb.at[0], recv_sem=vb.at[0],
+                device_id={"band": partner}, device_id_type=MESH)
+            pair.start()
+            sends.append(pair)
+            own_ref[...] = land[...]
+        if q == parts - 1:
+            pair.wait_recv()
+            b2[x] = land[...] + b1[...]
+            for o in range(1, chips):
+                to = lax.rem(x + o, chips)
+                copy = pltpu.make_async_remote_copy(
+                    src_ref=b2.at[x], dst_ref=b2.at[x], send_sem=sc.at[o], recv_sem=vc.at[o],
+                    device_id={"band": to * 2 + core}, device_id_type=MESH)
+                copy.start()
+                sends.append(copy)
         for o in range(1, chips):
             frm = lax.rem(x - o + chips, chips)
             pltpu.make_async_remote_copy(
@@ -341,12 +358,21 @@
     for o in range(1, bands):
         frm = lax.rem(me - o + bands, bands)
         pltpu.make_async_remote_copy(
-            src_ref=a_ref, dst_ref=ar.at[frm], send_sem=sa.at[o], recv_sem=va.at[o],
+            src_ref=a_ref.at[pl.ds(0, SUB)], dst_ref=ar.at[frm], send_sem=sa.at[o], recv_sem=va.at[o],
             device_id={"band": frm}, device_id_type=MESH).wait_recv()
     total = ar[0]
     for i in range(1, bands):
         total = total + ar[i]
     aout_ref[...] = total
+    for o in range(1, chips):
+        frm = lax.rem(x - o + chips, chips)
+        pltpu.make_async_remote_copy(
+            src_ref=b2.at[frm], dst_ref=b2.at[frm], send_sem=sc.at[o], recv_sem=vc.at[o],
+            device_id={"band": frm * 2 + core}, device_id_type=MESH).wait_recv()
+    total = b2[0]
+    for i in range(1, chips):
+        total = total + b2[i]
+    sum_ref[...] = total
     for q in range(parts):
         last[q].wait_recv()
         gout_ref[:, chunk(1 - core, q), :] = r3[q]
@@ -354,39 +380,56 @@
         copy.wait_send()
 
 
-def band_sum(grad, auxt, bands, cid):
+def band_sum(packets, grad, aux, tiles, bands, cid):
     sources, pixels, lanes = grad.shape
     parts = 4
     rows = pixels // 2 // parts
     chips = bands // 2
     dma = pltpu.SemaphoreType.DMA
     return pl.pallas_call(
-        functools.partial(reduce_kernel, bands, parts),
-        out_shape=[jax.ShapeDtypeStruct(grad.shape, F32), jax.ShapeDtypeStruct(auxt.shape, F32)],
-        in_specs=[VM, VM], out_specs=[VM, VM],
+        functools.partial(reduce_kernel, tiles, bands, parts),
+        out_shape=[jax.ShapeDtypeStruct(grad.shape, F32), jax.ShapeDtypeStruct((SUB, lanes), F32),
+                   jax.ShapeDtypeStruct(packets.shape, F32), jax.ShapeDtypeStruct(packets.shape, F32)],
+        in_specs=[VM] * 3, out_specs=[VM] * 4,
         scratch_shapes=[pltpu.VMEM((parts, sources, rows, lanes), F32),
                         pltpu.VMEM((chips, parts, sources, rows, lanes), F32),
                         pltpu.VMEM((parts, sources, rows, lanes), F32),
-                        pltpu.VMEM((bands,) + auxt.shape, F32),
+                        pltpu.VMEM((bands, SUB, lanes), F32),
+                        pltpu.VMEM(packets.shape, F32), pltpu.VMEM(packets.shape, F32),
+                        pltpu.VMEM((chips,) + packets.shape, F32),
                         dma((parts,)), dma((parts,)), dma((chips, parts)), dma((chips, parts)),
-                        dma((parts,)), dma((parts,)), dma((bands,)), dma((bands,))],
+                        dma((parts,)), dma((parts,)), dma((bands,)), dma((bands,)), dma((tiles,)), dma((tiles,)),
+                        dma((1,)), dma((1,)), dma((chips,)), dma((chips,))],
         compiler_params=pltpu.CompilerParams(collective_id=cid, has_side_effects=True),
-    )(grad, auxt)
-
-
-def step_kernel(final, sent_ref, shape_ref, grad_ref, auxt_ref, cntb_ref, memt_ref, color_ref, *outs):
+    )(packets, grad, aux)
+
+
+def step_kernel(final, chan, sent_ref, shape_ref, grad_ref, auxt_ref, cntb_ref, memt_ref, color_ref,
+                sum_ref, own_ref, pb_ref, aux_ref, amask_ref, snext_ref, cnext_ref, *outs):
     sources = shape_ref.shape[0]
-    snext_ref = outs[0]
+    slots = sum_ref.shape[0]
+    sent = sent_ref[...][:slots]
+    memt = memt_ref[...]
+    per_block = pb_ref[...] + select_dot(own_ref[:, sources, :], sent, TN)
+    grad_color = select_dot(per_block, memt, NN)
+    powers = select_dot(aux_ref[pl.ds(SUB, SUB), :], memt, NN)
+    row = lax.broadcasted_iota(jnp.int32, color_ref.shape, 0) // chan
+    power = jnp.zeros(color_ref.shape, F32)
+    for k in range(sources):
+        power = jnp.where(row == k, powers[k:k + 1], power)
+    color = jnp.maximum(color_ref[...] - grad_color / (1.0 + power), 0.0) * amask_ref[...]
+    cnext_ref[...] = color
     for k in range(sources):
         step = 1.0 / (1.0 + auxt_ref[pl.ds(k, 1), :])
         alive = jnp.where(cntb_ref[pl.ds(0, 1), :] > k, 1.0, 0.0)
-        shape = jnp.maximum(shape_ref[k] - step * grad_ref[k], 0.0) * alive
+        grad = grad_ref[k] + select_dot(sum_ref[:, k, :], sent, TN)
+        shape = jnp.maximum(shape_ref[k] - step * grad, 0.0) * alive
         snext_ref[k] = jnp.transpose(shape) if final else shape
     if final:
-        outs[1][...] = select_dot(auxt_ref[...], memt_ref[...], NN)
+        outs[0][...] = select_dot(auxt_ref[...], memt, NN)
     else:
-        outs[1][...] = select_dot(color_ref[...], memt_ref[...], NT)
-        write_packets(sent_ref, snext_ref, outs[1], outs[2])
+        outs[0][...] = select_dot(color, memt, NT)
+        write_packets(sent_ref, snext_ref, outs[0], outs[1])
 
 
 def on_device(
@@ -417,25 +460,23 @@
         out_shape=[turned, palette, table, sds((blocks, blends), BF), sds((SUB, blocks), F32), palette, packet],
     )(sent, morphology, spec2, blend_blocks, source_count.reshape(1, blends))
     for it in range(ITERS):
-        recv = exchange(packets, tiles, 3 * it)
+        recv = exchange(packets, tiles, 2 * it)
         grad, pb, aux, ret = main_pass(hit, recv, observed, weights, shape_now, cb)
-        back = exchange(ret, tiles, 3 * it + 1)
-        grad, auxt, color_now = pl.pallas_call(
-            functools.partial(fix_kernel, chan),
-            in_specs=[VM] * 8, out_specs=[VM] * 3,
-            out_shape=[turned, sds((SUB, blocks), F32), palette],
-        )(sent, back, grad, pb, aux, memt, color_now, amask)
-        grad, auxt = band_sum(grad, auxt, bands, 3 * it + 2)
+        grad, auxt, back_sum, back = band_sum(ret, grad, aux, tiles, bands, 2 * it + 1)
         final = it == ITERS - 1
-        outs = [sds(morphology.shape, F32), sds((SUB, blends), F32)] if final else [turned, table, packet]
+        if final:
+            outs = [sds(morphology.shape, F32), palette, sds((SUB, blends), F32)]
+        else:
+            outs = [turned, palette, table, packet]
         results = pl.pallas_call(
-            functools.partial(step_kernel, final),
-            in_specs=[VM] * 7, out_specs=[VM] * len(outs), out_shape=outs,
-        )(sent, shape_now, grad, auxt, cntb, memt, color_now)
+            functools.partial(step_kernel, final, chan),
+            in_specs=[VM] * 12, out_specs=[VM] * len(outs), out_shape=outs,
+        )(sent, shape_now, grad, auxt, cntb, memt, color_now, back_sum, back, pb, aux, amask)
+        color_now = results[1]
         if not final:
-            shape_now, cb, packets = results
+            shape_now, _, cb, packets = results
     spectra_out = color_now[:sources * chan].reshape(sources, chan, blends)
-    return (results[0], spectra_out, results[1][sources])
+    return (results[0], spectra_out, results[2][sources])
 
 
 def solution(mesh):

time: 134 us -> 119 us (0.89)
  Pallas kernels: 126 us -> 110 us
    pallas_call x4 -> x2, Pallas kernels: 38.3 us -> 19.2 us  [exchange(): pl.pallas_call(functools.partial(exchange_kernel, tiles), out_shape=jax.S...]
    pallas_call x6 -> x4, Pallas kernels: 50.9 us -> 54.8 us  [the longest x2 46.5 us: band_sum(): pl.pallas_call(functools.partial(reduce_kernel, tiles, bands, parts), out...]
where the time goes in v1:
time: 119 us
  Pallas kernels  110 us (92%)
  local copies, waits for them, and re-layouts  6.04 us (5%)
  other arithmetic  1.48 us (1%)
    pallas_call x2, Pallas kernels, band_sum(): pl.pallas_call(functools.partial(reduce_kernel, tiles, bands, parts), out...  46.5 us
    pallas_call x2, Pallas kernels, main_pass(): pl.pallas_call(functools.partial(main_kernel, sources), grid=(blocks // r...  33.3 us
    pallas_call x2, Pallas kernels, exchange(): pl.pallas_call(functools.partial(exchange_kernel, tiles), out_shape=jax.S...  19.2 us
    pallas_call x2, Pallas kernels, on_device(): pl.pallas_call(functools.partial(step_kernel, final, chan), in_specs=[VM]...  8.33 us
    pallas_call x1, Pallas kernels, on_device(): pl.pallas_call(functools.partial(start_kernel, chan), in_specs=[VM] * 5,...  3.09 us

profile of v1, /device:TPU:0, one launch (start us, length us, event | category | flops | bytes accessed | tf_op | source)
XLA Modules:
  0.0 118.7 jit_solution(13061874296513932750)
XLA Ops:
  0.6 0.8 copy.13
  1.4 0.1 reshape.23
  1.5 0.8 copy.14
  2.2 0.1 reshape.26
  2.3 0.7 fusion.sent_ref
  3.1 0.7 fusion.1.hit_ref
  3.8 1.6 %pad.12.spec_ref = f32[128,256]{1,0:T(8,128)} pad(f32[96,256]{1,0:T(8,128)} %bitcast.4, f32[]{:T(128)} %constant.4.clone.1), padding=0_32x0_0 | pad | bytes 229380 | tf_op jit(solution)/shard_map/jit(_pad)/pad | solution.py:451
  5.4 3.1 %shard_map.103 = (f32[4,128,512]{2,1,0:T(8,128)}, f32[128,256]{1,0:T(8,128)}, f32[128,512]{1,0:T(8,128)}, bf16[512,256]{1,0:T(8,128)(2,1)}, f32[8,512]{1,0:T(8,1...) custom-call(bf16[128,512]{1,0:T(8,128)(2,1)} %fusion.sent_ref, f32[4,512,128]{2,1,0:T(8,128)} %morph_ref.1, ...), custom_call_target="tpu_custom_call" | custom-call | tf_op jit(solution)/shard_map/pallas_call | solution.py:457
  8.5 10.9 %shard_map.104.recv_ref = f32[32,8,128]{2,1,0:T(8,128)} custom-call(f32[32,8,128]{2,1,0:T(8,128)} %get-tuple-element.34.src_ref), custom_call_target="tpu_custom_call" | custom-call | tf_op jit(solution)/shard_map/pallas_call | solution.py:118
  19.4 16.6 %shard_map.105 = (f32[4,128,512]{2,1,0:T(8,128)}, f32[128,512]{1,0:T(8,128)}, f32[16,512]{1,0:T(8,128)}, f32[32,8,128]{2,1,0:T(8,128)}) custom-call(bf16[128,512]{1,0:T(8,128)(2,1)} %fusion.1.hit_ref, f32[32,8,128]{2,1,0:T(8,128)} %shard_map.104.recv_ref, f32[24,512,128]{2,1,0:T(8,128)} %obs_ref.3, f32[24,512,128]{2,1,0:T(8,128)} %wts_ref.3, ...), custom_call_target="tpu_custom_call" | custom-call | tf_op jit(solution)/shard_map/pallas_call | solution.py:248
  36.0 24.4 %shard_map.106 = (f32[4,128,512]{2,1,0:T(8,128)}, f32[8,512]{1,0:T(8,128)}, f32[32,8,128]{2,1,0:T(8,128)}, f32[32,8,128]{2,1,0:T(8,128)}) custom-call(f32[32,8,128]{2,1,0:T(8,128)} %get-tuple-element.36.src_ref, f32[4,128,512]{2,1,0:T(8,128)} %get-tuple-element.37.g_ref, f32[16,512]{1,0:T(8,128)} %get-tuple-element.38.a_ref.aux_ref), custom_call_target="tpu_custom_call" | custom-call | tf_op jit(solution)/shard_map/pallas_call | solution.py:389
  60.4 4.3 %shard_map.107 = (f32[4,128,512]{2,1,0:T(8,128)}, f32[128,256]{1,0:T(8,128)}, f32[128,512]{1,0:T(8,128)}, f32[32,8,128]{2,1,0:T(8,128)}) custom-call(bf16[128,512]{1,0:T(8,128)(2,1)} %fusion.sent_ref, f32[4,128,512]{2,1,0:T(8,128)} %get-tuple-element.33.shape_ref, f32[4,128,512]{2,1,0:T(8,128)} %get-tuple-element.39.grad_ref, ...), custom_call_target="tpu_custom_call" | custom-call | tf_op jit(solution)/shard_map/pallas_call | solution.py:471
  64.7 8.3 %shard_map.108.recv_ref = f32[32,8,128]{2,1,0:T(8,128)} custom-call(f32[32,8,128]{2,1,0:T(8,128)} %get-tuple-element.49.src_ref), custom_call_target="tpu_custom_call" | custom-call | tf_op jit(solution)/shard_map/pallas_call | solution.py:118
  73.1 16.6 %shard_map.109 = (f32[4,128,512]{2,1,0:T(8,128)}, f32[128,512]{1,0:T(8,128)}, f32[16,512]{1,0:T(8,128)}, f32[32,8,128]{2,1,0:T(8,128)}) custom-call(bf16[128,512]{1,0:T(8,128)(2,1)} %fusion.1.hit_ref, f32[32,8,128]{2,1,0:T(8,128)} %shard_map.108.recv_ref, f32[24,512,128]{2,1,0:T(8,128)} %obs_ref.3, f32[24,512,128]{2,1,0:T(8,128)} %wts_ref.3, ...), custom_call_target="tpu_custom_call" | custom-call | tf_op jit(solution)/shard_map/pallas_call | solution.py:248
  89.7 22.1 %shard_map.110 = (f32[4,128,512]{2,1,0:T(8,128)}, f32[8,512]{1,0:T(8,128)}, f32[32,8,128]{2,1,0:T(8,128)}, f32[32,8,128]{2,1,0:T(8,128)}) custom-call(f32[32,8,128]{2,1,0:T(8,128)} %get-tuple-element.51.src_ref, f32[4,128,512]{2,1,0:T(8,128)} %get-tuple-element.52.g_ref, f32[16,512]{1,0:T(8,128)} %get-tuple-element.53.a_ref.aux_ref), custom_call_target="tpu_custom_call" | custom-call | tf_op jit(solution)/shard_map/pallas_call | solution.py:389
  111.8 4.1 %shard_map.111 = (f32[4,512,128]{2,1,0:T(8,128)}, f32[128,256]{1,0:T(8,128)}, f32[8,256]{1,0:T(8,128)}) custom-call(bf16[128,512]{1,0:T(8,128)(2,1)} %fusion.sent_ref, f32[4,128,512]{2,1,0:T(8,128)} %get-tuple-element.48.shape_ref, f32[4,128,512]{2,1,0:T(8,128)} %get-tuple-element.54.grad_ref, f32[8,512]{1,0:T(8,128)} %get-tuple-element.55.auxt_ref, ...), custom_call_target="tpu_custom_call" | custom-call | tf_op jit(solution)/shard_map/pallas_call | solution.py:471
  115.9 1.3 %slice.7 = f32[1,256]{1,0:T(1,128)} slice(f32[8,256]{1,0:T(8,128)} %get-tuple-element.62), slice={[4:5], [0:256]} | slice | bytes 2048 | tf_op jit(solution)/shard_map/slice | solution.py:479
  117.1 1.5 %slice.6 = f32[96,256]{1,0:T(8,128)} slice(f32[128,256]{1,0:T(8,128)} %get-tuple-element.61), slice={[0:96], [0:256]} | slice | bytes 196608 | tf_op jit(solution)/shard_map/slice | solution.py:478
  (2 shorter events, 0.0 us)
